TPU v7x, 32 devices: a whole 2x2x4 slice. The times are simulated.
32 devices in a mesh: grp: 2 (over y), dp: 16 (over z, x, core).
Axes of the slice: x: 2, y: 2, z: 4, core: 2. Of those that a mesh axis runs over, the one named last changes fastest.
Arguments:
- hidden_in: bfloat16 [2, 64, 4096], P(None, ('grp', 'dp')), parts along dimension 1, may hold values from -6 to 6
- norm_gain: float32 [4096], replicated, may hold values from 0.1 to 1.9
- queries: bfloat16 [2, 64, 4096], P(None, ('grp', 'dp')), parts along dimension 1, may hold values from -72 to 72
- new_keys: bfloat16 [2, 64, 1024], P(None, ('grp', 'dp')), parts along dimension 1, may hold values from -9 to 9
- new_values: bfloat16 [2, 64, 1024], P(None, ('grp', 'dp')), parts along dimension 1, may hold values from -6 to 6
- cache_keys: bfloat16 [64, 384, 1024], P(('grp', 'dp')), parts along dimension 0, may hold values from -9 to 9
- cache_values: bfloat16 [64, 384, 1024], P(('grp', 'dp')), parts along dimension 0, may hold values from -6 to 6
- lengths: int32 [64], P(('grp', 'dp')), parts along dimension 0, may hold values from 1 to 384
- routes: int32 [2, 64, 2], P(None, ('grp', 'dp')), parts along dimension 1, may hold values from 0 to 3, all different within a row; in each aligned block of 2 rows (0 to 1, 2 to 3, ..., all dimensions but the last counted through in order) at most 2 rows name the same one
- gate_logits: float32 [2, 64, 2], P(None, ('grp', 'dp')), parts along dimension 1, may hold values from -6 to 6
- w_gate: bfloat16 [28672, 4096], P('dp'), may hold values from -0.09375 to 0.09375
- w_up: bfloat16 [28672, 4096], P('dp'), may hold values from -0.09375 to 0.09375
- w_down: bfloat16 [28672, 4096], P('dp'), may hold values from -0.0625 to 0.0625
Outputs:
- hidden_out: bfloat16 [2, 64, 4096], P(None, ('grp', 'dp')), parts along dimension 1
There are 2 independent parts, one for each index of `grp`. A program takes and returns all parts, laid end to end along the dimension named above; an argument that names none is the same for every part. Nothing has to cross between parts.
Inputs may be any that keep to these rules, and one draw needn't show every extreme that they name: `routes`: each token names 2 different experts. Among the 2 tokens of one device at one decoded position no expert is named more than 2 times, a bound that some block reaches.
All inputs are finite; a program needn't handle non-finite values.
Results may differ from a plain program's by a relative error of at most 0.0055.
Values may be sent and summed in bfloat16 or wider, within the bound.
A program may use at most 192 MiB of HBM per device.

v0:
```python
import functools

import jax
import jax.numpy as jnp
from jax import lax
from jax.experimental import pallas as pl
from jax.experimental.pallas import tpu as pltpu
from jax.sharding import PartitionSpec as P

HEAD_DIM = 128
EXPERTS = 4
PAD = 16
MESH = pl.DeviceIdType.MESH
F32 = jnp.float32
BF16 = jnp.bfloat16
NEG = -1e30
PARTS = ((2, False), (1, False), (1, True), (1, True), (1, True), (1, True), (1, True))
ROWS_BY_ROWS = (((1,), (1,)), ((), ()))
COLS_BY_ROWS = (((0,), (0,)), ((), ()))


def kernel(
    n,
    pieces,
    parts,
    lengths_hbm,
    routes_hbm,
    logits_hbm,
    hidden_hbm,
    gain_hbm,
    q_hbm,
    nk_hbm,
    nv_hbm,
    ck_hbm,
    cv_hbm,
    wg_hbm,
    wu_hbm,
    wd_hbm,
    out_ref,
    lengths_ref,
    routes_ref,
    logits_ref,
    hidden_ref,
    gain_ref,
    q_ref,
    nk_ref,
    nv_ref,
    kvbuf,
    wgu,
    wd,
    qs,
    bias,
    carried,
    blocks,
    xs,
    xb,
    ssq,
    acc_g,
    acc_u,
    act,
    part,
    s1,
    r1,
    s2,
    r2,
    s3,
    r3,
    s4,
    r4,
    sem_in,
    sem_kv,
    sem_gu,
    sem_d,
    sem_a,
    sem_c,
    sem_r,
    sem_s,
):
    new, docs, width = hidden_ref.shape
    tokens = new * docs
    cache_len, kv_width = ck_hbm.shape[1], ck_hbm.shape[2]
    kv_heads = kv_width // HEAD_DIM
    group = width // kv_width
    hidden = wg_hbm.shape[0]
    pair = 2
    nc = kv_heads // pair
    ck = width // nc
    nk = len(parts)
    relayed = [k for k, (_, _, direct) in enumerate(parts) if not direct]
    straight = [k for k, (_, _, direct) in enumerate(parts) if direct]
    quads = n // 4
    rows = n * tokens
    half = rows // 2
    score_scale = HEAD_DIM ** (-0.5)

    grp, me = lax.axis_index("grp"), lax.axis_index("dp")
    core = lax.rem(me, 2)
    xbit = lax.rem(me // 2, 2)
    quad = me // 4
    core_dev = (grp, me + 1 - 2 * core)
    x_dev = (grp, me + 2 - 4 * xbit)

    def quad_dev(d):
        return (grp, lax.rem(quad + d, quads) * 4 + lax.rem(me, 4))

    def diagonal_dev(d):
        return (grp, lax.rem(quad + d, quads) * 4 + lax.rem(me, 4) + 2 - 4 * xbit)

    barrier = pltpu.get_barrier_semaphore()
    order = [d for i in range(quads // 2, 0, -1) for d in dict.fromkeys([i, quads - i])]
    chips = [dev(d) for d in order for dev in (diagonal_dev, quad_dev)] + [x_dev]
    for dev in chips + [core_dev]:
        pl.semaphore_signal(barrier, inc=1, device_id=dev, device_id_type=MESH)

    smalls = [
        (q_hbm, q_ref),
        (nk_hbm, nk_ref),
        (nv_hbm, nv_ref),
        (lengths_hbm, lengths_ref),
        (hidden_hbm, hidden_ref),
        (gain_hbm, gain_ref),
        (routes_hbm, routes_ref),
        (logits_hbm, logits_ref),
    ]
    small_copies = [
        pltpu.make_async_copy(src, dst, sem_in.at[i]) for i, (src, dst) in enumerate(smalls)
    ]

    def lanes_of(c):
        return pl.ds(c * pair * HEAD_DIM, pair * HEAD_DIM)

    def cache_rows(c):
        return kvbuf.at[:, :, pl.ds(0, cache_len), lanes_of(c)]

    def cache_copies(c):
        return [
            pltpu.make_async_copy(src.at[:, :, lanes_of(c)], cache_rows(c).at[i], sem_kv.at[c])
            for i, src in enumerate((ck_hbm, cv_hbm))
        ]

    for copy in small_copies[:5] + cache_copies(0) + small_copies[5:]:
        copy.start()
    for c in range(1, nc):
        for copy in cache_copies(c):
            copy.start()

    def start_weights():
        for p, (at, size, _) in enumerate(pieces):
            for i, src in enumerate((wg_hbm, wu_hbm)):
                lanes = pl.ds(at, size)
                pltpu.make_async_copy(src.at[:, lanes], wgu.at[i, :, lanes], sem_gu.at[p]).start()
        pltpu.make_async_copy(wd_hbm, wd, sem_d.at[0]).start()

    with jax.named_scope("inwait"):
        for copy in small_copies[:5]:
            copy.wait()
    for t in range(new):
        q32 = q_ref[t].astype(F32)
        for head in range(kv_heads * group):
            qs[head * tokens + t * docs : head * tokens + (t + 1) * docs, :] = q32[
                :, head * HEAD_DIM : (head + 1) * HEAD_DIM
            ]
        carried[t * docs : (t + 1) * docs, :] = hidden_ref[t].astype(F32)
    extra = lax.broadcasted_iota(jnp.int32, (PAD, kv_width), 0)
    for i, src in enumerate((nk_ref, nv_ref)):
        for d in range(docs):
            value = jnp.zeros((PAD, kv_width), F32)
            for u in range(new):
                value = jnp.where(extra == u, src[u, d : d + 1].astype(F32), value)
            kvbuf[i, d, cache_len : cache_len + PAD, :] = value.astype(BF16)
    prow = pair * group * tokens
    row = lax.broadcasted_iota(jnp.int32, (prow, cache_len + PAD), 0)
    col = lax.broadcasted_iota(jnp.int32, (prow, cache_len + PAD), 1)
    row_doc = lax.rem(row, docs)
    row_new = lax.rem(row, tokens) // docs
    limit = jnp.zeros_like(row)
    for d in range(docs):
        limit = jnp.where(row_doc == d, lengths_ref[d], limit)
    keep = (col < limit) | ((col >= cache_len) & (col - cache_len <= row_new))
    keep = jnp.logical_and(keep, (col < cache_len) | (col < cache_len + new))
    bias[...] = jnp.where(keep, 0.0, NEG)

    def block_copy(p, index, count, send_sem, recv_sem, dev):
        ref = blocks.at[pl.ds(index, count), :, pl.ds(pieces[p][0], pieces[p][1])]
        return pltpu.make_async_remote_copy(
            src_ref=ref,
            dst_ref=ref,
            send_sem=sem_s.at[send_sem],
            recv_sem=recv_sem.at[p],
            device_id=dev,
            device_id_type=MESH,
        )

    mine = (core * 2 + xbit) * quads + quad

    def core_copy(p, z):
        index = lax.rem(core + z, 2) * 2 * quads
        return block_copy(p, index, 2 * quads, 1, sem_c, core_dev)

    def scores_of(c):
        zeros = jnp.zeros((group * tokens, HEAD_DIM), F32)
        lines = []
        for i in range(pair):
            h = c * pair + i
            q = qs[h * group * tokens : (h + 1) * group * tokens, :]
            lines.append(jnp.concatenate([zeros] * i + [q] + [zeros] * (pair - 1 - i), axis=1))
        q = jnp.concatenate(lines, axis=0).astype(BF16)
        lanes = slice(c * pair * HEAD_DIM, (c + 1) * pair * HEAD_DIM)
        value = None
        for d in range(docs):
            s = lax.dot_general(
                q, kvbuf[0, d, :, lanes], ROWS_BY_ROWS, preferred_element_type=F32
            )
            value = s if d == 0 else jnp.where(row_doc == d, s, value)
        return value

    def context_of(c, value):
        value = value * score_scale + bias[...]
        e = jnp.exp(value - jnp.max(value, axis=1, keepdims=True))
        p = e * (1.0 / jnp.sum(e, axis=1, keepdims=True))
        lanes = slice(c * pair * HEAD_DIM, (c + 1) * pair * HEAD_DIM)
        result = None
        for d in range(docs):
            r = jnp.dot(
                jnp.where(row_doc == d, p, 0.0).astype(BF16),
                kvbuf[1, d, :, lanes],
                preferred_element_type=F32,
            )
            result = r if d == 0 else result + r
        pieces = []
        for i in range(pair):
            for g in range(group):
                at = (i * group + g) * tokens
                pieces.append(result[at : at + tokens, i * HEAD_DIM : (i + 1) * HEAD_DIM])
        return jnp.concatenate(pieces, axis=1)

    def wait_cache(c):
        with jax.named_scope(f"kv{c}"):
            pltpu.make_async_copy(cache_rows(c), cache_rows(c), sem_kv.at[c]).wait()

    def attend(c, value):
        with jax.named_scope(f"attn{c}"):
            lanes = slice(c * ck, (c + 1) * ck)
            car = carried[:, lanes] + context_of(c, value)
            carried[:, lanes] = car
            blocks[mine, :, lanes] = car.astype(BF16)

    def send_chunk(c):
        for p, (_, _, chunk) in enumerate(pieces):
            if chunk == c:
                for dev in chips:
                    block_copy(p, mine, 1, 0, sem_a, dev).start()

    wait_cache(0)
    attend(0, scores_of(0))
    with jax.named_scope("bar"):
        pl.semaphore_wait(barrier, 2 * quads)
    send_chunk(0)
    for c in range(1, nc):
        wait_cache(c)
    start_weights()
    with jax.named_scope("scores1"):
        values = [scores_of(c) for c in range(1, nc)]
    for c in range(1, nc):
        attend(c, values[c - 1])
        send_chunk(c)
    for copy in small_copies[5:]:
        copy.wait()

    def forward(p):
        with jax.named_scope(f"A{p}"):
            block_copy(p, 0, 2 * quads - 1, 0, sem_a, core_dev).wait_recv()
            core_copy(p, 0).start()

    def gather(p):
        at, size, _ = pieces[p]
        lanes = slice(at, at + size)
        with jax.named_scope(f"C{p}"):
            core_copy(p, 1).wait_recv()
        for b in range(n):
            xs[b * tokens : (b + 1) * tokens, 0:size] = blocks[b, :, lanes].astype(F32)
        value = xs[:, 0:size]
        square = value * value
        total = square[:, 0:HEAD_DIM]
        for i in range(1, size // HEAD_DIM):
            total = total + square[:, i * HEAD_DIM : (i + 1) * HEAD_DIM]
        ssq[...] = total if p == 0 else ssq[...] + total
        xb[:, lanes] = (value * gain_ref[:, lanes]).astype(BF16)

    nh = 2
    hc = hidden // nh

    def gate_up(p, j, scale):
        rows_at = slice(j * hc, (j + 1) * hc)
        lanes = slice(pieces[p][0], pieces[p][0] + pieces[p][1])
        x = xb[:, lanes]
        g = lax.dot_general(wgu[0, rows_at, lanes], x, ROWS_BY_ROWS, preferred_element_type=F32)
        u = lax.dot_general(wgu[1, rows_at, lanes], x, ROWS_BY_ROWS, preferred_element_type=F32)
        if p > 0:
            g = g + acc_g[rows_at, :]
            u = u + acc_u[rows_at, :]
        if p < len(pieces) - 1:
            acc_g[rows_at, :] = g
            acc_u[rows_at, :] = u
        else:
            g = g * scale
            act[rows_at, :] = (g * jax.nn.sigmoid(g) * (u * scale)).astype(BF16)

    forward(0)
    for p, (at, size, _) in enumerate(pieces):
        gather(p)
        scale = None
        if p == len(pieces) - 1:
            total = jnp.sum(jnp.transpose(ssq[...]), axis=0, keepdims=True)
            scale = lax.rsqrt(total / width + 1e-05)
        with jax.named_scope(f"guwait{p}"):
            ref = wgu.at[:, :, pl.ds(at, size)]
            pltpu.make_async_copy(ref, ref, sem_gu.at[p]).wait()
        for j in range(nh):
            with jax.named_scope(f"gu{p}"):
                gate_up(p, j, scale)
            if j == 0 and p < len(pieces) - 1:
                forward(p + 1)

    def pair_copy(src, dst, stage, k, dev):
        return pltpu.make_async_remote_copy(
            src_ref=src,
            dst_ref=dst,
            send_sem=sem_s.at[2 + stage],
            recv_sem=sem_r.at[min(stage, 2), k],
            device_id=dev,
            device_id_type=MESH,
        )

    def lanes_at(k):
        return pl.ds(parts[k][0], parts[k][1])

    copy_1 = [
        pair_copy(s1.at[1 - core, :, lanes_at(k)], r1.at[:, lanes_at(k)], 0, k, core_dev)
        for k in range(nk)
    ]
    copy_2 = {
        k: pair_copy(s2.at[1 - xbit, :, lanes_at(k)], r2.at[:, lanes_at(k)], 1, k, x_dev)
        for k in relayed
    }
    others = pl.ds(0, quads - 1)
    rest = pl.ds(0, 2 * quads - 1)

    def sends_3(k):
        lanes = lanes_at(k)
        return [
            pair_copy(
                s3.at[lax.rem(quad + d, quads), :, lanes], r3.at[quad, :, lanes], 2, k, quad_dev(d)
            )
            for d in range(1, quads)
        ]

    def sends_4(k):
        lanes = lanes_at(k)
        here = r4.at[xbit * quads + quad, :, lanes]
        copies = []
        for d in order:
            to = lax.rem(quad + d, quads)
            for x, dev in ((1 - xbit, diagonal_dev(d)), (xbit, quad_dev(d))):
                copies.append(pair_copy(s4.at[x * quads + to, :, lanes], here, 3, k, dev))
        copies.append(pair_copy(s4.at[(1 - xbit) * quads + quad, :, lanes], here, 3, k, x_dev))
        return copies

    def start_1(k):
        at, size, _ = parts[k]
        lanes = slice(at, at + size)
        with jax.named_scope(f"down{k}"):
            value = lax.dot_general(act[...], wd[:, lanes], COLS_BY_ROWS, preferred_element_type=F32)
            s1[0, :, lanes] = value[:half].astype(BF16)
            s1[1, :, lanes] = value[half:].astype(BF16)
        copy_1[k].start()

    def start_2(k):
        at, size, direct = parts[k]
        lanes = slice(at, at + size)
        with jax.named_scope(f"r1wait{k}"):
            copy_1[k].wait_recv()
        value = s1[core, :, lanes].astype(F32) + r1[:, lanes].astype(F32)
        if direct:
            for i in range(2 * quads):
                s4[i, :, lanes] = value[i * tokens : (i + 1) * tokens].astype(BF16)
            own = xbit * quads + quad
            r4[own, :, lanes] = s4[own, :, lanes]
            for copy in sends_4(k):
                copy.start()
        else:
            value = value.astype(BF16)
            s2[0, :, lanes] = value[: half // 2]
            s2[1, :, lanes] = value[half // 2 :]
            copy_2[k].start()

    def start_3(k):
        at, size, _ = parts[k]
        lanes = slice(at, at + size)
        with jax.named_scope(f"r2wait{k}"):
            copy_2[k].wait_recv()
        part[:, 0:size] = s2[xbit, :, lanes].astype(F32) + r2[:, lanes].astype(F32)
        for q in range(quads):
            s3[q, :, lanes] = part[q * tokens : (q + 1) * tokens, 0:size].astype(BF16)
        r3[quad, :, lanes] = s3[quad, :, lanes]
        for copy in sends_3(k):
            copy.start()

    token = lax.broadcasted_iota(jnp.int32, (tokens, 1), 0)
    margin = jnp.zeros((tokens, 1), F32)
    first = jnp.zeros((tokens, 1), jnp.int32)
    second = jnp.zeros((tokens, 1), jnp.int32)
    for t in range(new):
        for d in range(docs):
            here = token == t * docs + d
            margin = jnp.where(here, logits_ref[t, d, 0] - logits_ref[t, d, 1], margin)
            first = jnp.where(here, routes_ref[t, d, 0], first)
            second = jnp.where(here, routes_ref[t, d, 1], second)
    share_a = jax.nn.sigmoid(margin)
    share_b = 1.0 - share_a
    share = [
        jnp.where(first == e, share_a, 0.0) + jnp.where(second == e, share_b, 0.0)
        for e in range(EXPERTS)
    ]

    def finish(k):
        at, size, direct = parts[k]
        lanes = slice(at, at + size)
        with jax.named_scope(f"r3wait{k}"):
            if direct:
                pair_copy(
                    s4.at[rest, :, lanes_at(k)], r4.at[rest, :, lanes_at(k)], 3, k, core_dev
                ).wait_recv()
            else:
                pair_copy(
                    s3.at[others, :, lanes_at(k)], r3.at[others, :, lanes_at(k)], 2, k, core_dev
                ).wait_recv()
        acc = carried[:, lanes]
        per = quads // EXPERTS
        for e in range(EXPERTS):
            if direct:
                got = [r4[x * quads + e * per + i, :, lanes] for x in range(2) for i in range(per)]
            else:
                got = [r3[e * per + i, :, lanes] for i in range(per)]
            value = got[0].astype(F32)
            for more in got[1:]:
                value = value + more.astype(F32)
            acc = acc + share[e] * value
        for t in range(new):
            out_ref[t, :, lanes] = acc[t * docs : (t + 1) * docs].astype(out_ref.dtype)

    with jax.named_scope("dwait"):
        pltpu.make_async_copy(wd_hbm, wd, sem_d.at[0]).wait()
    lag = min(2, nk)
    for k in range(nk):
        start_1(k)
        if k >= lag:
            start_2(k - lag)
    for k in range(nk - lag, nk):
        start_2(k)
    for k in relayed:
        start_3(k)
    for k in range(nk):
        finish(k)

    def span(indices):
        at = parts[indices[0]][0]
        return pl.ds(at, parts[indices[-1]][0] + parts[indices[-1]][1] - at)

    with jax.named_scope("sends"):
        sent = [blocks.at[rest], blocks.at[pl.ds(0, 2 * quads)], r1]
        sent += [r2.at[:, span(relayed)], s3.at[others, :, span(relayed)]] if relayed else [None] * 2
        sent += [s4.at[rest, :, span(straight)]] if straight else []
        for i, ref in enumerate(sent):
            if ref is None:
                continue
            pltpu.make_async_remote_copy(
                src_ref=ref,
                dst_ref=ref,
                send_sem=sem_s.at[i],
                recv_sem=sem_s.at[i],
                device_id=core_dev,
                device_id_type=MESH,
            ).wait_send()


def per_device(
    hidden_in,
    norm_gain,
    queries,
    new_keys,
    new_values,
    cache_keys,
    cache_values,
    lengths,
    routes,
    gate_logits,
    w_gate,
    w_up,
    w_down,
):
    n = lax.axis_size("dp")
    new, docs, width = hidden_in.shape
    tokens = new * docs
    rows = n * tokens
    hidden = w_gate.shape[0]
    cache_len, kv_width = cache_keys.shape[1:]
    kv_heads = kv_width // HEAD_DIM
    group = width // kv_width
    quads = n // 4
    chunk = 2 * HEAD_DIM * group
    pieces = [(0, chunk // 2, 0), (chunk // 2, chunk // 2, 0)]
    pieces += [(c * chunk, chunk, c) for c in range(1, width // chunk)]
    parts, at = [], 0
    for size, direct in PARTS:
        parts.append((at * width // 8, size * width // 8, direct))
        at += size
    vmem = pl.BlockSpec(memory_space=pltpu.VMEM)
    hbm = pl.BlockSpec(memory_space=pl.ANY)
    dma = pltpu.SemaphoreType.DMA
    return pl.pallas_call(
        functools.partial(kernel, n, pieces, parts),
        out_shape=pltpu.VMEM(hidden_in.shape, BF16),
        in_specs=[hbm] * 13,
        out_specs=vmem,
        scratch_shapes=[
            pltpu.SMEM(lengths.shape, jnp.int32),
            pltpu.SMEM(routes.shape, jnp.int32),
            pltpu.SMEM(gate_logits.shape, F32),
            pltpu.VMEM(hidden_in.shape, BF16),
            pltpu.VMEM((1, width), F32),
            pltpu.VMEM(queries.shape, BF16),
            pltpu.VMEM(new_keys.shape, BF16),
            pltpu.VMEM(new_values.shape, BF16),
            pltpu.VMEM((2, docs, cache_len + PAD, kv_width), BF16),
            pltpu.VMEM((2, hidden, width), BF16),
            pltpu.VMEM((hidden, width), BF16),
            pltpu.VMEM((kv_heads * group * tokens, HEAD_DIM), F32),
            pltpu.VMEM((2 * group * tokens, cache_len + PAD), F32),
            pltpu.VMEM((tokens, width), F32),
            pltpu.VMEM((n, tokens, width), BF16),
            pltpu.VMEM((rows, chunk), F32),
            pltpu.VMEM((rows, width), BF16),
            pltpu.VMEM((rows, HEAD_DIM), F32),
            pltpu.VMEM((hidden, rows), F32),
            pltpu.VMEM((hidden, rows), F32),
            pltpu.VMEM((hidden, rows), BF16),
            pltpu.VMEM((rows // 4, chunk), F32),
            pltpu.VMEM((2, rows // 2, width), BF16),
            pltpu.VMEM((rows // 2, width), BF16),
            pltpu.VMEM((2, rows // 4, width), BF16),
            pltpu.VMEM((rows // 4, width), BF16),
            pltpu.VMEM((quads, tokens, width), BF16),
            pltpu.VMEM((quads, tokens, width), BF16),
            pltpu.VMEM((2 * quads, tokens, width), BF16),
            pltpu.VMEM((2 * quads, tokens, width), BF16),
            dma((8,)),
            dma((kv_heads // 2,)),
            dma((len(pieces),)),
            dma((1,)),
            dma((len(pieces),)),
            dma((len(pieces),)),
            dma((3, len(parts))),
            dma((6,)),
        ],
        compiler_params=pltpu.CompilerParams(
            collective_id=0, has_side_effects=True, vmem_limit_bytes=66000000
        ),
        name="decode_layer",
    )(
        lengths,
        routes,
        gate_logits,
        hidden_in,
        norm_gain.reshape(1, width),
        queries,
        new_keys,
        new_values,
        cache_keys,
        cache_values,
        w_gate,
        w_up,
        w_down,
    )


def solution(mesh):
    in_specs = (
        P(None, ("grp", "dp"), None),
        P(),
        P(None, ("grp", "dp"), None),
        P(None, ("grp", "dp"), None),
        P(None, ("grp", "dp"), None),
        P(("grp", "dp"), None, None),
        P(("grp", "dp"), None, None),
        P(("grp", "dp")),
        P(None, ("grp", "dp"), None),
        P(None, ("grp", "dp"), None),
        P("dp", None),
        P("dp", None),
        P("dp", None),
    )
    out_specs = P(None, ("grp", "dp"), None)
    return jax.shard_map(
        per_device, mesh=mesh, in_specs=in_specs, out_specs=out_specs, check_vma=False
    )
```

profile of v0, /device:TPU:0, one launch (start us, length us, event | category | flops | bytes accessed | tf_op | source)
XLA Modules:
  0.0 31.6 jit_solution(6198300760745650802)
XLA Ops:
  0.0 31.0 %decode_layer.1 = bf16[2,2,4096]{2,1,0:T(2,128)(2,1)S(1)} custom-call(s32[2]{0:T(128)} %lengths_hbm.1, s32[2,2,2]{2,1,0:T(2,128)} %routes_hbm.1, f32[2,2,2]{2,1,0:T(2,128)} %logits_hbm.1, bf16[2,2,4096]{2,1,0:T(2,128)(2,1)} %hidden_hbm.1, f32[1,4096]{1,0:T(1,128)} %bitcast.1, bf16[2,2,4096]{2,1,0:T(2,128)(2,1)} %q_hbm.1, bf16[2,2,1024]{2,1,0:T(2,128)(2,1)} %nk_hbm.1, ...), custom_call_target="tpu_custom_call" | custom-call | tf_op jit(solution)/shard_map/decode_layer/pallas_call | solution.py:521
  31.0 0.6 %copy.15 = bf16[2,2,4096]{2,1,0:T(2,128)(2,1)} copy(bf16[2,2,4096]{2,1,0:T(2,128)(2,1)S(1)} %decode_layer.1) | data formatting | bytes 65536
where the time goes:
time: 31.8 us; the launch traced here: 31.6 us
  Pallas kernels  31 us (97%)
  local copies, waits for them, and re-layouts  0.62 us (2%)
    pallas_call x1, Pallas kernels, per_device(): pl.pallas_call(functools.partial(kernel, n, pieces, parts), out_shape=plt...  31 us

commit v1 on v0

--- a/solution.py
+++ b/solution.py
@@ -100,16 +100,17 @@
     core_dev = (grp, me + 1 - 2 * core)
     x_dev = (grp, me + 2 - 4 * xbit)
 
-    def quad_dev(d):
-        return (grp, lax.rem(quad + d, quads) * 4 + lax.rem(me, 4))
-
-    def diagonal_dev(d):
-        return (grp, lax.rem(quad + d, quads) * 4 + lax.rem(me, 4) + 2 - 4 * xbit)
-
+    def opposite(x, d):
+        at_x = xbit if x == 0 else 1 - xbit
+        return (grp, lax.rem(quad + d, quads) * 4 + at_x * 2 + 1 - core)
+
+    def back(d):
+        return (quads - d) % quads
+
+    order = [d for i in range(quads // 2, 0, -1) for d in dict.fromkeys([i, quads - i])] + [0]
+    chips = [(x, d) for d in order for x in (1, 0)]
     barrier = pltpu.get_barrier_semaphore()
-    order = [d for i in range(quads // 2, 0, -1) for d in dict.fromkeys([i, quads - i])]
-    chips = [dev(d) for d in order for dev in (diagonal_dev, quad_dev)] + [x_dev]
-    for dev in chips + [core_dev]:
+    for dev in [opposite(x, d) for x, d in chips] + [x_dev]:
         pl.semaphore_signal(barrier, inc=1, device_id=dev, device_id_type=MESH)
 
     smalls = [
@@ -180,22 +181,19 @@
     keep = jnp.logical_and(keep, (col < cache_len) | (col < cache_len + new))
     bias[...] = jnp.where(keep, 0.0, NEG)
 
-    def block_copy(p, index, count, send_sem, recv_sem, dev):
-        ref = blocks.at[pl.ds(index, count), :, pl.ds(pieces[p][0], pieces[p][1])]
+    def block_copy(p, src, dst, count, send_sem, recv_sem, dev):
+        lanes = pl.ds(pieces[p][0], pieces[p][1])
         return pltpu.make_async_remote_copy(
-            src_ref=ref,
-            dst_ref=ref,
+            src_ref=blocks.at[pl.ds(src, count), :, lanes],
+            dst_ref=blocks.at[pl.ds(dst, count), :, lanes],
             send_sem=sem_s.at[send_sem],
             recv_sem=recv_sem.at[p],
             device_id=dev,
             device_id_type=MESH,
         )
 
-    mine = (core * 2 + xbit) * quads + quad
-
-    def core_copy(p, z):
-        index = lax.rem(core + z, 2) * 2 * quads
-        return block_copy(p, index, 2 * quads, 1, sem_c, core_dev)
+    mine = core * 2 * quads
+    theirs = (1 - core) * 2 * quads
 
     def scores_of(c):
         zeros = jnp.zeros((group * tokens, HEAD_DIM), F32)
@@ -248,17 +246,18 @@
     def send_chunk(c):
         for p, (_, _, chunk) in enumerate(pieces):
             if chunk == c:
-                for dev in chips:
-                    block_copy(p, mine, 1, 0, sem_a, dev).start()
+                for x, d in chips:
+                    slot = mine + x * quads + back(d)
+                    block_copy(p, mine, slot, 1, 0, sem_a, opposite(x, d)).start()
 
     wait_cache(0)
     attend(0, scores_of(0))
+    start_weights()
     with jax.named_scope("bar"):
-        pl.semaphore_wait(barrier, 2 * quads)
+        pl.semaphore_wait(barrier, 2 * quads + 1)
     send_chunk(0)
     for c in range(1, nc):
         wait_cache(c)
-    start_weights()
     with jax.named_scope("scores1"):
         values = [scores_of(c) for c in range(1, nc)]
     for c in range(1, nc):
@@ -269,14 +268,14 @@
 
     def forward(p):
         with jax.named_scope(f"A{p}"):
-            block_copy(p, 0, 2 * quads - 1, 0, sem_a, core_dev).wait_recv()
-            core_copy(p, 0).start()
+            block_copy(p, theirs, theirs, 2 * quads, 0, sem_a, core_dev).wait_recv()
+            block_copy(p, theirs + 1, theirs + 1, 2 * quads - 1, 1, sem_c, core_dev).start()
 
     def gather(p):
         at, size, _ = pieces[p]
         lanes = slice(at, at + size)
         with jax.named_scope(f"C{p}"):
-            core_copy(p, 1).wait_recv()
+            block_copy(p, mine + 1, mine + 1, 2 * quads - 1, 1, sem_c, core_dev).wait_recv()
         for b in range(n):
             xs[b * tokens : (b + 1) * tokens, 0:size] = blocks[b, :, lanes].astype(F32)
         value = xs[:, 0:size]
@@ -306,7 +305,8 @@
             g = g * scale
             act[rows_at, :] = (g * jax.nn.sigmoid(g) * (u * scale)).astype(BF16)
 
-    forward(0)
+    for p in range(2):
+        forward(p)
     for p, (at, size, _) in enumerate(pieces):
         gather(p)
         scale = None
@@ -319,8 +319,8 @@
         for j in range(nh):
             with jax.named_scope(f"gu{p}"):
                 gate_up(p, j, scale)
-            if j == 0 and p < len(pieces) - 1:
-                forward(p + 1)
+        if p + 2 < len(pieces):
+            forward(p + 2)
 
     def pair_copy(src, dst, stage, k, dev):
         return pltpu.make_async_remote_copy(
@@ -336,35 +336,33 @@
         return pl.ds(parts[k][0], parts[k][1])
 
     copy_1 = [
-        pair_copy(s1.at[1 - core, :, lanes_at(k)], r1.at[:, lanes_at(k)], 0, k, core_dev)
+        pair_copy(s1.at[core, :, lanes_at(k)], r1.at[:, lanes_at(k)], 0, k, core_dev)
         for k in range(nk)
     ]
     copy_2 = {
-        k: pair_copy(s2.at[1 - xbit, :, lanes_at(k)], r2.at[:, lanes_at(k)], 1, k, x_dev)
+        k: pair_copy(s2.at[1, :, lanes_at(k)], r2.at[:, lanes_at(k)], 1, k, x_dev)
         for k in relayed
     }
-    others = pl.ds(0, quads - 1)
-    rest = pl.ds(0, 2 * quads - 1)
 
     def sends_3(k):
         lanes = lanes_at(k)
         return [
-            pair_copy(
-                s3.at[lax.rem(quad + d, quads), :, lanes], r3.at[quad, :, lanes], 2, k, quad_dev(d)
-            )
-            for d in range(1, quads)
+            pair_copy(s3.at[d, :, lanes], r3.at[back(d), :, lanes], 2, k, opposite(0, d))
+            for d in order
         ]
 
     def sends_4(k):
         lanes = lanes_at(k)
-        here = r4.at[xbit * quads + quad, :, lanes]
-        copies = []
-        for d in order:
-            to = lax.rem(quad + d, quads)
-            for x, dev in ((1 - xbit, diagonal_dev(d)), (xbit, quad_dev(d))):
-                copies.append(pair_copy(s4.at[x * quads + to, :, lanes], here, 3, k, dev))
-        copies.append(pair_copy(s4.at[(1 - xbit) * quads + quad, :, lanes], here, 3, k, x_dev))
-        return copies
+        return [
+            pair_copy(
+                s4.at[x * quads + d, :, lanes],
+                r4.at[x * quads + back(d), :, lanes],
+                3,
+                k,
+                opposite(x, d),
+            )
+            for x, d in chips
+        ]
 
     def start_1(k):
         at, size, _ = parts[k]
@@ -380,12 +378,10 @@
         lanes = slice(at, at + size)
         with jax.named_scope(f"r1wait{k}"):
             copy_1[k].wait_recv()
-        value = s1[core, :, lanes].astype(F32) + r1[:, lanes].astype(F32)
+        value = s1[1 - core, :, lanes].astype(F32) + r1[:, lanes].astype(F32)
         if direct:
             for i in range(2 * quads):
                 s4[i, :, lanes] = value[i * tokens : (i + 1) * tokens].astype(BF16)
-            own = xbit * quads + quad
-            r4[own, :, lanes] = s4[own, :, lanes]
             for copy in sends_4(k):
                 copy.start()
         else:
@@ -399,10 +395,9 @@
         lanes = slice(at, at + size)
         with jax.named_scope(f"r2wait{k}"):
             copy_2[k].wait_recv()
-        part[:, 0:size] = s2[xbit, :, lanes].astype(F32) + r2[:, lanes].astype(F32)
+        part[:, 0:size] = s2[0, :, lanes].astype(F32) + r2[:, lanes].astype(F32)
         for q in range(quads):
             s3[q, :, lanes] = part[q * tokens : (q + 1) * tokens, 0:size].astype(BF16)
-        r3[quad, :, lanes] = s3[quad, :, lanes]
         for copy in sends_3(k):
             copy.start()
 
@@ -418,34 +413,26 @@
             second = jnp.where(here, routes_ref[t, d, 1], second)
     share_a = jax.nn.sigmoid(margin)
     share_b = 1.0 - share_a
-    share = [
-        jnp.where(first == e, share_a, 0.0) + jnp.where(second == e, share_b, 0.0)
-        for e in range(EXPERTS)
-    ]
+    share = []
+    for d in range(quads):
+        e = lax.rem(quad + d, quads) // (quads // EXPERTS)
+        share.append(jnp.where(first == e, share_a, 0.0) + jnp.where(second == e, share_b, 0.0))
 
     def finish(k):
         at, size, direct = parts[k]
         lanes = slice(at, at + size)
         with jax.named_scope(f"r3wait{k}"):
+            src, dst = (s4, r4) if direct else (s3, r3)
+            pair_copy(
+                src.at[:, :, lanes_at(k)], dst.at[:, :, lanes_at(k)], 3 if direct else 2, k, core_dev
+            ).wait_recv()
+        acc = carried[:, lanes]
+        for d in range(quads):
             if direct:
-                pair_copy(
-                    s4.at[rest, :, lanes_at(k)], r4.at[rest, :, lanes_at(k)], 3, k, core_dev
-                ).wait_recv()
+                value = r4[d, :, lanes].astype(F32) + r4[quads + d, :, lanes].astype(F32)
             else:
-                pair_copy(
-                    s3.at[others, :, lanes_at(k)], r3.at[others, :, lanes_at(k)], 2, k, core_dev
-                ).wait_recv()
-        acc = carried[:, lanes]
-        per = quads // EXPERTS
-        for e in range(EXPERTS):
-            if direct:
-                got = [r4[x * quads + e * per + i, :, lanes] for x in range(2) for i in range(per)]
-            else:
-                got = [r3[e * per + i, :, lanes] for i in range(per)]
-            value = got[0].astype(F32)
-            for more in got[1:]:
-                value = value + more.astype(F32)
-            acc = acc + share[e] * value
+                value = r3[d, :, lanes].astype(F32)
+            acc = acc + share[d] * value
         for t in range(new):
             out_ref[t, :, lanes] = acc[t * docs : (t + 1) * docs].astype(out_ref.dtype)
 
@@ -468,12 +455,9 @@
         return pl.ds(at, parts[indices[-1]][0] + parts[indices[-1]][1] - at)
 
     with jax.named_scope("sends"):
-        sent = [blocks.at[rest], blocks.at[pl.ds(0, 2 * quads)], r1]
-        sent += [r2.at[:, span(relayed)], s3.at[others, :, span(relayed)]] if relayed else [None] * 2
-        sent += [s4.at[rest, :, span(straight)]] if straight else []
+        sent = [blocks.at[pl.ds(0, 2 * quads)], blocks.at[pl.ds(0, 2 * quads - 1)], r1]
+        sent += [r2.at[:, span(relayed)], s3.at[:, :, span(relayed)], s4.at[:, :, span(straight)]]
         for i, ref in enumerate(sent):
-            if ref is None:
-                continue
             pltpu.make_async_remote_copy(
                 src_ref=ref,
                 dst_ref=ref,

time: 31.8 us -> 29.9 us (0.940)
  Pallas kernels: 31 us -> 29.2 us
    pallas_call x1, Pallas kernels: 31 us -> 29.2 us  [per_device(): pl.pallas_call(functools.partial(kernel, n, pieces, parts), out_shape=plt...]
where the time goes in v1:
time: 29.9 us; the launch traced here: 29.8 us
  Pallas kernels  29.2 us (98%)
  local copies, waits for them, and re-layouts  0.62 us (2%)
    pallas_call x1, Pallas kernels, per_device(): pl.pallas_call(functools.partial(kernel, n, pieces, parts), out_shape=plt...  29.2 us
    unnamed x1, local copies, waits for them, and re-layouts  0.62 us

profile of v1, /device:TPU:0, one launch (start us, length us, event | category | flops | bytes accessed | tf_op | source)
XLA Modules:
  0.0 29.8 jit_solution(5223678170064155641)
XLA Ops:
  0.0 29.2 %decode_layer.1 = bf16[2,2,4096]{2,1,0:T(2,128)(2,1)S(1)} custom-call(s32[2]{0:T(128)} %lengths_hbm.1, s32[2,2,2]{2,1,0:T(2,128)} %routes_hbm.1, f32[2,2,2]{2,1,0:T(2,128)} %logits_hbm.1, bf16[2,2,4096]{2,1,0:T(2,128)(2,1)} %hidden_hbm.1, f32[1,4096]{1,0:T(1,128)} %bitcast.1, bf16[2,2,4096]{2,1,0:T(2,128)(2,1)} %q_hbm.1, bf16[2,2,1024]{2,1,0:T(2,128)(2,1)} %nk_hbm.1, ...), custom_call_target="tpu_custom_call" | custom-call | tf_op jit(solution)/shard_map/decode_layer/pallas_call | solution.py:505
  29.2 0.6 %copy.15 = bf16[2,2,4096]{2,1,0:T(2,128)(2,1)} copy(bf16[2,2,4096]{2,1,0:T(2,128)(2,1)S(1)} %decode_layer.1) | data formatting | bytes 65536

commit v2 on v1

--- a/solution.py
+++ b/solution.py
@@ -14,7 +14,7 @@
 F32 = jnp.float32
 BF16 = jnp.bfloat16
 NEG = -1e30
-PARTS = ((2, False), (1, False), (1, True), (1, True), (1, True), (1, True), (1, True))
+PARTS = ((2, False), (1, True), (1, True), (1, True), (1, True), (1, True), (1, True))
 ROWS_BY_ROWS = (((1,), (1,)), ((), ()))
 COLS_BY_ROWS = (((0,), (0,)), ((), ()))
 
@@ -139,7 +139,7 @@
             for i, src in enumerate((ck_hbm, cv_hbm))
         ]
 
-    for copy in small_copies[:5] + cache_copies(0) + small_copies[5:]:
+    for copy in cache_copies(0) + small_copies:
         copy.start()
     for c in range(1, nc):
         for copy in cache_copies(c):
@@ -327,7 +327,7 @@
             src_ref=src,
             dst_ref=dst,
             send_sem=sem_s.at[2 + stage],
-            recv_sem=sem_r.at[min(stage, 2), k],
+            recv_sem=sem_r.at[(0, 2 * nk, nk, nk)[stage] + k],
             device_id=dev,
             device_id_type=MESH,
         )
@@ -447,7 +447,7 @@
         start_2(k)
     for k in relayed:
         start_3(k)
-    for k in range(nk):
+    for k in straight + relayed:
         finish(k)
 
     def span(indices):
@@ -544,7 +544,7 @@
             dma((1,)),
             dma((len(pieces),)),
             dma((len(pieces),)),
-            dma((3, len(parts))),
+            dma((3 * len(parts) - sum(direct for _, _, direct in parts),)),
             dma((6,)),
         ],
         compiler_params=pltpu.CompilerParams(

time: 29.9 us -> 29.6 us (0.990)
  Pallas kernels: 29.2 us -> 28.8 us
    pallas_call x1, Pallas kernels: 29.2 us -> 28.8 us  [per_device(): pl.pallas_call(functools.partial(kernel, n, pieces, parts), out_shape=plt...]
where the time goes in v2:
time: 29.6 us; the launch traced here: 29.4 us
  Pallas kernels  28.8 us (97%)
  local copies, waits for them, and re-layouts  0.62 us (2%)
    pallas_call x1, Pallas kernels, per_device(): pl.pallas_call(functools.partial(kernel, n, pieces, parts), out_shape=plt...  28.8 us
    unnamed x1, local copies, waits for them, and re-layouts  0.62 us

profile of v2, /device:TPU:0, one launch (start us, length us, event | category | flops | bytes accessed | tf_op | source)
XLA Modules:
  0.0 29.4 jit_solution(2684823777144903770)
XLA Ops:
  0.0 28.8 %decode_layer.1 = bf16[2,2,4096]{2,1,0:T(2,128)(2,1)S(1)} custom-call(s32[2]{0:T(128)} %lengths_hbm.1, s32[2,2,2]{2,1,0:T(2,128)} %routes_hbm.1, f32[2,2,2]{2,1,0:T(2,128)} %logits_hbm.1, bf16[2,2,4096]{2,1,0:T(2,128)(2,1)} %hidden_hbm.1, f32[1,4096]{1,0:T(1,128)} %bitcast.1, bf16[2,2,4096]{2,1,0:T(2,128)(2,1)} %q_hbm.1, bf16[2,2,1024]{2,1,0:T(2,128)(2,1)} %nk_hbm.1, ...), custom_call_target="tpu_custom_call" | custom-call | tf_op jit(solution)/shard_map/decode_layer/pallas_call | solution.py:505
  28.8 0.6 %copy.15 = bf16[2,2,4096]{2,1,0:T(2,128)(2,1)} copy(bf16[2,2,4096]{2,1,0:T(2,128)(2,1)S(1)} %decode_layer.1) | data formatting | bytes 65536
